TPU v7x, 32 devices: a whole 2x2x4 slice. The times are simulated.
32 devices in a mesh: tok: 8 (over z, y), vocab: 4 (over x, core).
Axes of the slice: x: 2, y: 2, z: 4, core: 2. Of those that a mesh axis runs over, the one named last changes fastest.
Arguments:
- hidden: bfloat16 [192, 9216], P('tok'), may hold values from -256 to 256
- policy_head: bfloat16 [9216, 32768], P(None, ('tok', 'vocab')), may hold values from -0.0625 to 0.0625
- reference_head: bfloat16 [9216, 32768], P(None, ('tok', 'vocab')), may hold values from -0.0625 to 0.0625
- targets: int32 [192], P('tok'), may hold values from 0 to 32767
Outputs:
- policy_logprob: float32 [192], P('tok')
- reference_logprob: float32 [192], P('tok')
- divergence: float32 [192], P('tok')
All inputs are finite; a program needn't handle non-finite values.
Results may differ from a plain program's by a relative error of at most 0.00055.
Values may be sent and summed in bfloat16 or wider, within the bound.
A program may use at most 128 MiB of HBM per device.

v0:
```python
import jax
import jax.numpy as jnp
from jax import lax
from jax.sharding import PartitionSpec as P


def combined_all(value, axis, combine):
    everything = jax.tree.map(lambda part: lax.all_gather(part, axis), value)
    leading = jax.tree.map(lambda part: part[0], everything)

    def step(k, so_far):
        return combine(so_far, jax.tree.map(lambda part: part[k], everything))

    return lax.fori_loop(1, lax.axis_size(axis), step, leading)


def local_sums(policy_logits, reference_logits, target_hits, peak_policy, peak_reference):
    policy_exp = jnp.exp(policy_logits - peak_policy[:, None])
    reference_exp = jnp.exp(reference_logits - peak_reference[:, None])
    total_policy = jnp.sum(policy_exp, axis=1)
    total_reference = jnp.sum(reference_exp, axis=1)
    weighted = jnp.sum(policy_exp * (policy_logits - reference_logits), axis=1)
    target_policy = jnp.sum(jnp.where(target_hits, policy_logits, 0.0), axis=1)
    target_reference = jnp.sum(jnp.where(target_hits, reference_logits, 0.0), axis=1)
    return (total_policy, total_reference, weighted, target_policy, target_reference)


def local_stats(policy_logits, reference_logits, target_hits):
    peak_policy = jnp.max(policy_logits, axis=1)
    peak_reference = jnp.max(reference_logits, axis=1)
    summed = local_sums(policy_logits, reference_logits, target_hits, peak_policy, peak_reference)
    return (peak_policy, peak_reference) + summed


def combine_stats(left_stats, right_stats):
    peak_policy = jnp.maximum(left_stats[0], right_stats[0])
    peak_reference = jnp.maximum(left_stats[1], right_stats[1])
    left_policy = jnp.exp(left_stats[0] - peak_policy)
    right_policy = jnp.exp(right_stats[0] - peak_policy)
    left_reference = jnp.exp(left_stats[1] - peak_reference)
    right_reference = jnp.exp(right_stats[1] - peak_reference)
    return (
        peak_policy,
        peak_reference,
        left_stats[2] * left_policy + right_stats[2] * right_policy,
        left_stats[3] * left_reference + right_stats[3] * right_reference,
        left_stats[4] * left_policy + right_stats[4] * right_policy,
        left_stats[5] + right_stats[5],
        left_stats[6] + right_stats[6],
    )


def combine_senders(received):
    peak_policy = jnp.max(received[0], axis=0)
    peak_reference = jnp.max(received[1], axis=0)
    policy_scale = jnp.exp(received[0] - peak_policy[None, :])
    reference_scale = jnp.exp(received[1] - peak_reference[None, :])
    return (
        peak_policy,
        peak_reference,
        jnp.sum(received[2] * policy_scale, axis=0),
        jnp.sum(received[3] * reference_scale, axis=0),
        jnp.sum(received[4] * policy_scale, axis=0),
        jnp.sum(received[5], axis=0),
        jnp.sum(received[6], axis=0),
    )


def finish(merged_stats):
    log_norm_policy = merged_stats[0] + jnp.log(merged_stats[2])
    log_norm_reference = merged_stats[1] + jnp.log(merged_stats[3])
    policy_logprob = merged_stats[5] - log_norm_policy
    reference_logprob = merged_stats[6] - log_norm_reference
    divergence = merged_stats[4] / merged_stats[2] - log_norm_policy + log_norm_reference
    return (policy_logprob, reference_logprob, divergence)


def body(hidden, policy_head, reference_head, targets):
    tok_count = lax.axis_size("tok")
    vocab_count = lax.axis_size("vocab")
    tok_rows = hidden.shape[0]
    vocab_cols = policy_head.shape[1]
    piece = lax.all_gather(hidden, "tok", axis=0, tiled=True)
    summed = jnp.concatenate(
        [
            jnp.dot(piece, policy_head, preferred_element_type=jnp.float32),
            jnp.dot(piece, reference_head, preferred_element_type=jnp.float32),
        ],
        axis=1,
    )
    policy_logits = summed[:, :vocab_cols]
    reference_logits = summed[:, vocab_cols:]
    every_target = lax.all_gather(targets, "tok", axis=0, tiled=True)
    block_index = lax.axis_index("tok") * vocab_count + lax.axis_index("vocab")
    vocab_ids = block_index * vocab_cols + lax.iota(jnp.int32, vocab_cols)
    target_hits = vocab_ids[None, :] == every_target[:, None]
    partial_value = local_stats(policy_logits, reference_logits, target_hits)
    shaped = tuple((entry.reshape(tok_count, tok_rows) for entry in partial_value))
    received = lax.all_to_all(shaped, "tok", split_axis=0, concat_axis=0, tiled=True)
    own_stats = combine_senders(received)
    merged_stats = combined_all(own_stats, "vocab", combine_stats)
    return finish(merged_stats)


def solution(mesh):
    in_specs = (P("tok", None), P(None, ("tok", "vocab")), P(None, ("tok", "vocab")), P("tok"))
    out_specs = (P("tok"), P("tok"), P("tok"))
    return jax.shard_map(body, mesh=mesh, in_specs=in_specs, out_specs=out_specs, check_vma=False)
```

profile of v0, /device:TPU:0, one launch (start us, length us, event | category | flops | bytes accessed | tf_op | source)
XLA Modules:
  0.0 179.8 jit_solution(15287167651976823062)
XLA Ops:
  7.2 0.0 all-gather.9.cloned.1.call-start
  7.2 0.7 all-gather.9.cloned.1.call-update
  7.9 1.2 dynamic-slice.5
  9.8 0.9 dynamic-update-slice.5
  10.7 13.1 %all-reduce.5 = s32[192]{0:T(256)S(1)} all-reduce(s32[192]{0:T(256)S(1)} %dynamic-update-slice.5), channel_id=1, replica_groups=mesh['tok'=8,'vocab'=4] {'tok'}, use_global_device_ids=true, to_apply=%add.5 | all-reduce | flops 192 | bytes 1536
  23.8 53.8 %all-gather.9.cloned.1.call-done = bf16[192,9216]{1,0:T(8,128)(2,1)} async-done(((bf16[24,9216]{1,0:T(8,128)(2,1)}), bf16[192,9216]{1,0:T(8,128)(2,1)}) %all-gather.9.cloned.1.call-update) | async-done | bytes 3538960 | tf_op jit(solution)/shard_map/all_gather | solution.py:83
  77.5 0.0 copy-start
  77.5 9.6 %fusion.24 = (f32[192]{0:T(256)S(1)}, f32[192,1024]{1,0:T(8,128)S(1)}) fusion(bf16[192,9216]{1,0:T(8,128)(2,1)} %all-gather.9.cloned.1.call-done, bf16[9216,1024]{1,0:T(8,128)(2,1)} %param.7), kind=kOutput, calls=%fused_computation.44 | convolution fusion | flops 3624075008 | bytes 23200512 | tf_op jit(solution)/shard_map/dot_general | solution.py:86
  87.2 3.1 %copy-done = bf16[9216,1024]{1,0:T(8,128)(2,1)S(1)} copy-done((bf16[9216,1024]{1,0:T(8,128)(2,1)S(1)}, bf16[9216,1024]{1,0:T(8,128)(2,1)}, u32[]{:S(2)}) %copy-start) | copy-done | bytes 18874392
  90.3 0.0 copy-start.1
  90.3 5.9 %fusion.25 = (f32[192]{0:T(256)S(1)}, f32[192,1024]{1,0:T(8,128)S(1)}) fusion(bf16[192,9216]{1,0:T(8,128)(2,1)} %all-gather.9.cloned.1.call-done, bf16[9216,1024]{1,0:T(8,128)(2,1)S(1)} %copy-done), kind=kOutput, calls=%fused_computation.45 | convolution fusion | flops 3624075008 | bytes 23200512 | tf_op jit(solution)/shard_map/dot_general | solution.py:87
  96.2 0.7 multiply_reduce_fusion
  96.9 0.7 all_to_all.64
  97.5 3.3 %all-to-all-start.4 = ((f32[8,1,24]{2,1,0:T(1,128)}), f32[8,1,24]{2,1,0:T(1,128)S(1)}, u32[]{:S(2)}, u32[]{:S(2)}) async-start(f32[8,1,24]{2,1,0:T(1,128)} %all_to_all.64), calls=%async_computation.4 | async-start | bytes 8192 | tf_op jit(solution)/shard_map/all_to_all | solution.py:99
  100.9 0.7 all_to_all.56
  101.6 5.8 %all-to-all-done.4 = f32[8,1,24]{2,1,0:T(1,128)S(1)} async-done(((f32[8,1,24]{2,1,0:T(1,128)}), f32[8,1,24]{2,1,0:T(1,128)S(1)}, u32[]{:S(2)}, u32[]{:S(2)}) %all-to-all-start.4) | async-done | bytes 800 | tf_op jit(solution)/shard_map/all_to_all | solution.py:99
  107.4 3.2 %all-to-all-start.2 = ((f32[8,1,24]{2,1,0:T(1,128)}), f32[8,1,24]{2,1,0:T(1,128)S(1)}, u32[]{:S(2)}, u32[]{:S(2)}) async-start(f32[8,1,24]{2,1,0:T(1,128)} %all_to_all.56), calls=%async_computation.2 | async-start | bytes 8192 | tf_op jit(solution)/shard_map/all_to_all | solution.py:99
  110.6 0.7 all_to_all.52
  111.3 5.7 %all-to-all-done.2 = f32[8,1,24]{2,1,0:T(1,128)S(1)} async-done(((f32[8,1,24]{2,1,0:T(1,128)}), f32[8,1,24]{2,1,0:T(1,128)S(1)}, u32[]{:S(2)}, u32[]{:S(2)}) %all-to-all-start.2) | async-done | bytes 800 | tf_op jit(solution)/shard_map/all_to_all | solution.py:99
  117.1 3.3 %all-to-all-start = ((f32[8,1,24]{2,1,0:T(1,128)}), f32[8,1,24]{2,1,0:T(1,128)S(1)}, u32[]{:S(2)}, u32[]{:S(2)}) async-start(f32[8,1,24]{2,1,0:T(1,128)} %all_to_all.52), calls=%async_computation | async-start | bytes 8192 | tf_op jit(solution)/shard_map/all_to_all | solution.py:99
  120.4 0.7 all_to_all.60
  121.1 5.8 %all-to-all-done = f32[8,1,24]{2,1,0:T(1,128)S(1)} async-done(((f32[8,1,24]{2,1,0:T(1,128)}), f32[8,1,24]{2,1,0:T(1,128)S(1)}, u32[]{:S(2)}, u32[]{:S(2)}) %all-to-all-start) | async-done | bytes 800 | tf_op jit(solution)/shard_map/all_to_all | solution.py:99
  126.8 3.2 %all-to-all-start.3 = ((f32[8,1,24]{2,1,0:T(1,128)}), f32[8,1,24]{2,1,0:T(1,128)S(1)}, u32[]{:S(2)}, u32[]{:S(2)}) async-start(f32[8,1,24]{2,1,0:T(1,128)} %all_to_all.60), calls=%async_computation.3 | async-start | bytes 8192 | tf_op jit(solution)/shard_map/all_to_all | solution.py:99
  130.1 0.7 all_to_all.54
  130.8 5.7 %all-to-all-done.3 = f32[8,1,24]{2,1,0:T(1,128)S(1)} async-done(((f32[8,1,24]{2,1,0:T(1,128)}), f32[8,1,24]{2,1,0:T(1,128)S(1)}, u32[]{:S(2)}, u32[]{:S(2)}) %all-to-all-start.3) | async-done | bytes 800 | tf_op jit(solution)/shard_map/all_to_all | solution.py:99
  136.5 3.3 %all-to-all-start.1 = ((f32[8,1,24]{2,1,0:T(1,128)}), f32[8,1,24]{2,1,0:T(1,128)S(1)}, u32[]{:S(2)}, u32[]{:S(2)}) async-start(f32[8,1,24]{2,1,0:T(1,128)} %all_to_all.54), calls=%async_computation.1 | async-start | bytes 8192 | tf_op jit(solution)/shard_map/all_to_all | solution.py:99
  139.9 0.0 copy-done.1
  139.9 0.6 dynamic-slice
  141.1 0.7 all_to_all.67
  141.8 0.7 all_to_all.69
  142.5 3.8 %all-to-all-done.1 = f32[8,1,24]{2,1,0:T(1,128)S(1)} async-done(((f32[8,1,24]{2,1,0:T(1,128)}), f32[8,1,24]{2,1,0:T(1,128)S(1)}, u32[]{:S(2)}, u32[]{:S(2)}) %all-to-all-start.1) | async-done | bytes 800 | tf_op jit(solution)/shard_map/all_to_all | solution.py:99
  146.3 3.2 %all-to-all-start.5 = ((f32[8,1,24]{2,1,0:T(1,128)}), f32[8,1,24]{2,1,0:T(1,128)S(1)}, u32[]{:S(2)}, u32[]{:S(2)}) async-start(f32[8,1,24]{2,1,0:T(1,128)} %all_to_all.67), calls=%async_computation.5 | async-start | bytes 8192 | tf_op jit(solution)/shard_map/all_to_all | solution.py:99
  149.6 6.4 %all-to-all-done.5 = f32[8,1,24]{2,1,0:T(1,128)S(1)} async-done(((f32[8,1,24]{2,1,0:T(1,128)}), f32[8,1,24]{2,1,0:T(1,128)S(1)}, u32[]{:S(2)}, u32[]{:S(2)}) %all-to-all-start.5) | async-done | bytes 800 | tf_op jit(solution)/shard_map/all_to_all | solution.py:99
  156.0 3.3 %all-to-all-start.6 = ((f32[8,1,24]{2,1,0:T(1,128)}), f32[8,1,24]{2,1,0:T(1,128)S(1)}, u32[]{:S(2)}, u32[]{:S(2)}) async-start(f32[8,1,24]{2,1,0:T(1,128)} %all_to_all.69), calls=%async_computation.6 | async-start | bytes 8192 | tf_op jit(solution)/shard_map/all_to_all | solution.py:99
  159.3 0.2 dynamic-update-slice
  159.5 0.2 dynamic-update-slice.1
  159.7 0.2 dynamic-update-slice.4
  159.9 0.2 dynamic-update-slice.2
  160.1 0.2 dynamic-update-slice.3
  160.4 0.2 dynamic-update-slice.6
  160.6 5.1 %all-to-all-done.6 = f32[8,1,24]{2,1,0:T(1,128)S(1)} async-done(((f32[8,1,24]{2,1,0:T(1,128)}), f32[8,1,24]{2,1,0:T(1,128)S(1)}, u32[]{:S(2)}, u32[]{:S(2)}) %all-to-all-start.6) | async-done | bytes 800 | tf_op jit(solution)/shard_map/all_to_all | solution.py:99
  165.7 0.2 dynamic-update-slice.7
  165.9 5.6 %all-reduce.8 = (f32[96]{0:T(128)S(1)}, f32[96]{0:T(128)S(1)}, f32[96]{0:T(128)S(1)}, f32[96]{0:T(128)S(1)}, f32[96]{0:T(128)S(1)}, /*index=5*/f32[96]{0:T(128)S(1)}, f32[96]{0:T(128)S(1)}) all-reduce(f32[96]{0:T(128)S(1)} %dynamic-update-slice, f32[96]{0:T(128)S(1)} %dynamic-update-slice.1, ...), channel_id=2, replica_groups=mesh['tok'=8,'vocab'=4] {'vocab'}, use_global_device_ids=true, to_apply=%add | all-reduce | flops 672 | bytes 5376
  171.6 0.1 reshape.43
  171.7 0.1 reshape.44
  171.7 0.1 reshape.45
  171.8 0.1 reshape.46
  171.9 0.1 reshape.47
  172.0 0.1 reshape.48
  172.1 0.1 reshape.49
  172.2 0.3 while.27
  172.5 0.5 subtract_add_fusion
  (27 shorter events, 0.4 us)
Async XLA Ops:
  7.2 70.3 %all-gather.9.cloned.1.call-start = ((), (), s32[]{:S(2)}) async-start(), calls=%async_computation.7 | async-start | bytes 3981312 | tf_op jit(solution)/shard_map/all_gather | solution.py:83
  77.5 12.7 %copy-start = (bf16[9216,1024]{1,0:T(8,128)(2,1)S(1)}, bf16[9216,1024]{1,0:T(8,128)(2,1)}, u32[]{:S(2)}) copy-start(bf16[9216,1024]{1,0:T(8,128)(2,1)} %param.8) | copy-start | bytes 56623108
  90.3 49.6 %copy-start.1 = (u32[32]{0:T(128)S(1)}, u32[32]{0:T(128)}, u32[]{:S(2)}) copy-start(u32[32]{0:T(128)} %constant.57) | copy-start | bytes 388
  97.5 9.8 %all-to-all-start.4 = ((f32[8,1,24]{2,1,0:T(1,128)}), f32[8,1,24]{2,1,0:T(1,128)S(1)}, u32[]{:S(2)}, u32[]{:S(2)}) async-start(f32[8,1,24]{2,1,0:T(1,128)} %all_to_all.64), calls=%async_computation.4 | async-start | bytes 8192 | tf_op jit(solution)/shard_map/all_to_all | solution.py:99
  107.4 9.7 %all-to-all-start.2 = ((f32[8,1,24]{2,1,0:T(1,128)}), f32[8,1,24]{2,1,0:T(1,128)S(1)}, u32[]{:S(2)}, u32[]{:S(2)}) async-start(f32[8,1,24]{2,1,0:T(1,128)} %all_to_all.56), calls=%async_computation.2 | async-start | bytes 8192 | tf_op jit(solution)/shard_map/all_to_all | solution.py:99
  117.1 9.8 %all-to-all-start = ((f32[8,1,24]{2,1,0:T(1,128)}), f32[8,1,24]{2,1,0:T(1,128)S(1)}, u32[]{:S(2)}, u32[]{:S(2)}) async-start(f32[8,1,24]{2,1,0:T(1,128)} %all_to_all.52), calls=%async_computation | async-start | bytes 8192 | tf_op jit(solution)/shard_map/all_to_all | solution.py:99
  126.8 9.7 %all-to-all-start.3 = ((f32[8,1,24]{2,1,0:T(1,128)}), f32[8,1,24]{2,1,0:T(1,128)S(1)}, u32[]{:S(2)}, u32[]{:S(2)}) async-start(f32[8,1,24]{2,1,0:T(1,128)} %all_to_all.60), calls=%async_computation.3 | async-start | bytes 8192 | tf_op jit(solution)/shard_map/all_to_all | solution.py:99
  136.5 9.8 %all-to-all-start.1 = ((f32[8,1,24]{2,1,0:T(1,128)}), f32[8,1,24]{2,1,0:T(1,128)S(1)}, u32[]{:S(2)}, u32[]{:S(2)}) async-start(f32[8,1,24]{2,1,0:T(1,128)} %all_to_all.54), calls=%async_computation.1 | async-start | bytes 8192 | tf_op jit(solution)/shard_map/all_to_all | solution.py:99
  146.3 9.7 %all-to-all-start.5 = ((f32[8,1,24]{2,1,0:T(1,128)}), f32[8,1,24]{2,1,0:T(1,128)S(1)}, u32[]{:S(2)}, u32[]{:S(2)}) async-start(f32[8,1,24]{2,1,0:T(1,128)} %all_to_all.67), calls=%async_computation.5 | async-start | bytes 8192 | tf_op jit(solution)/shard_map/all_to_all | solution.py:99
  156.0 9.7 %all-to-all-start.6 = ((f32[8,1,24]{2,1,0:T(1,128)}), f32[8,1,24]{2,1,0:T(1,128)S(1)}, u32[]{:S(2)}, u32[]{:S(2)}) async-start(f32[8,1,24]{2,1,0:T(1,128)} %all_to_all.69), calls=%async_computation.6 | async-start | bytes 8192 | tf_op jit(solution)/shard_map/all_to_all | solution.py:99
Sparse Core Ops, SparseCore 0:
  10.2 67.3 all-gather.8
where the time goes:
time: 180 us
  waiting for transfers between devices  92.7 us (52%)
  starting transfers between devices  23.1 us (13%)
  blocking collectives  18.7 us (10%)
  matrix products  15.6 us (9%)
  between operations  15.5 us (9%)
  local copies, waits for them, and re-layouts  12.7 us (7%)
    all_gather x1, waiting for transfers between devices, body(): piece = lax.all_gather(hidden, 'tok', axis=0, tiled=True)  53.8 us
    all_to_all x7, waiting for transfers between devices, body(): lax.all_to_all(shaped, 'tok', split_axis=0, concat_axis=0, tiled=True)  38.3 us
    all_to_all x7, starting transfers between devices, body(): lax.all_to_all(shaped, 'tok', split_axis=0, concat_axis=0, tiled=True)  23 us
    unnamed x2, blocking collectives  18.7 us
    dot_general x1, matrix products, body(): jnp.dot(piece, policy_head, preferred_element_type=jnp.float32)  9.63 us
    unnamed x22, local copies, waits for them, and re-layouts  7.34 us
    dot_general x1, matrix products, body(): jnp.dot(piece, reference_head, preferred_element_type=jnp.float32)  5.92 us
    all_to_all x7, local copies, waits for them, and re-layouts, body(): lax.all_to_all(shaped, 'tok', split_axis=0, concat_axis=0, tiled=True)  4.75 us
  transfers between devices with their start and end apart: 8, of which 8 were waited for; matrix products, arithmetic and copies ran while one was open for 2% of the time, Pallas kernels for 0%

commit v1 on v0

v1 whole, which is shorter than its diff:
```python
import functools

import jax
import jax.numpy as jnp
from jax import lax
from jax.experimental import pallas as pl
from jax.experimental.pallas import tpu as pltpu
from jax.sharding import PartitionSpec as P

MESH = pl.DeviceIdType.MESH
TILE = 256


def kernel(T, V, hid, wp, wr, tgt, o0, o1, o2, h, w, acc, tg, st, got,
           wsem, osem, rs, rr, xs, xr, cs, cr, ts, tr, es, er):
    R = hid.shape[0]
    D = hid.shape[1]
    C = wp.shape[1]
    M = T * R
    Kp = D // 6
    t = lax.axis_index("tok")
    v = lax.axis_index("vocab")
    core = lax.rem(v, 2)
    xb = lax.rem(v // 2, 2)
    partner = v + 1 - 2 * core
    twin = v + 2 - 4 * xb
    half = T // 2
    pos = jnp.where(lax.rem(t, 2) == 0, t // 2, T - 1 - t // 2)

    def tok_at(p):
        p = lax.rem(p + 2 * T, T)
        return jnp.where(p < half, 2 * p, 2 * (T - 1 - p) + 1)

    right, left = tok_at(pos + 1), tok_at(pos - 1)

    def part(c, kind):
        if kind == 0:
            return 3 * c
        return 3 * c + 1 + (xb if kind == 1 else 1 - xb)

    order = [(0, 0), (1, 0), (0, 1), (1, 1), (0, 2), (1, 2)]

    def cols(p):
        return pl.ds(pl.multiple_of(p * Kp, 128), Kp)

    own = pltpu.make_async_copy(hid, h.at[t], osem)
    own.start()
    wcopies = []
    for i, (c, kind) in enumerate(order):
        k = cols(part(c, kind))
        wcopies.append([
            pltpu.make_async_copy(wp.at[k, :], w.at[k, pl.ds(0, C)], wsem.at[0, i]),
            pltpu.make_async_copy(wr.at[k, :], w.at[k, pl.ds(C, C)], wsem.at[1, i]),
        ])

    barrier = pltpu.get_barrier_semaphore()

    def greet(j, _):
        q = lax.rem(t * V + v + j, T * V)
        pl.semaphore_signal(barrier, inc=1, device_id=(q // V, lax.rem(q, V)), device_id_type=MESH)
        return 0

    lax.fori_loop(1, T * V, greet, 0)
    for pair in wcopies:
        for cp in pair:
            cp.start()

    rowi = lax.broadcasted_iota(jnp.int32, (R, 128), 0)
    tv = jnp.zeros((R, 128), jnp.int32)
    for i in range(R):
        tv = jnp.where(rowi == i, tgt[i], tv)
    tg[t] = tv
    own.wait()
    pl.semaphore_wait(barrier, T * V - 1)

    counts = {(0, 0): half, (0, 1): T - 1 - half, (1, 0): T - 1 - half, (1, 1): half}
    sends = []

    def ring(kind, d, n):
        src = tok_at(pos - n) if d == 0 else tok_at(pos + n)
        blk = h.at[src, :, cols(part(core, kind))]
        return pltpu.make_async_remote_copy(
            src_ref=blk, dst_ref=blk, send_sem=rs.at[kind, d, n], recv_sem=rr.at[kind, d, n],
            device_id=(right if d == 0 else left, v), device_id_type=MESH)

    def landed(d, n):
        return tok_at(pos - 1 - n) if d == 0 else tok_at(pos + 1 + n)

    def cross(kind, d, n):
        blk = h.at[landed(d, n), :, cols(part(core, kind))]
        return pltpu.make_async_remote_copy(
            src_ref=blk, dst_ref=blk, send_sem=xs.at[d, n], recv_sem=xr.at[d, n],
            device_id=(t, twin), device_id_type=MESH)

    def pairwise(c, kind, dd, n):
        blk = h.at[landed(dd, n), :, cols(part(c, kind))]
        return pltpu.make_async_remote_copy(
            src_ref=blk, dst_ref=blk, send_sem=cs.at[kind, dd, n], recv_sem=cr.at[kind, dd, n],
            device_id=(t, partner), device_id_type=MESH)

    def go(cp):
        cp.start()
        sends.append(cp)

    xcounts = {0: counts[(1, 0)], 1: counts[(1, 1)]}

    for n in range(half + 1):
        for kind in (1, 0):
            for d in (0, 1):
                cnt = counts[(kind, d)]
                if 1 <= n <= cnt:
                    ring(kind, d, n - 1).wait_recv()
                if n < cnt:
                    go(ring(kind, d, n))
                if 1 <= n <= cnt:
                    if kind == 1:
                        go(cross(1, d, n - 1))
                    go(pairwise(core, kind, d, n - 1))
        if n == 0:
            for j in range(1, T):
                go(pltpu.make_async_remote_copy(
                    src_ref=tg.at[t], dst_ref=tg.at[t], send_sem=ts.at[j], recv_sem=tr.at[j],
                    device_id=(lax.rem(t + j, T), v), device_id_type=MESH))
        if n >= 3:
            for d in (0, 1):
                if n - 3 < xcounts[d]:
                    cross(2, d, n - 3).wait_recv()
                    go(pairwise(core, 2, d, n - 3))

    def matmul(i):
        c, kind = order[i]
        k = cols(part(c, kind))
        for cp in wcopies[i]:
            cp.wait()
        a = h[:, :, k].reshape(M, Kp)

        def tile(j, _):
            nn = pl.ds(pl.multiple_of(j * TILE, TILE), TILE)
            y = jnp.dot(a, w[k, nn], preferred_element_type=jnp.float32)
            if i == 0:
                acc[:, nn] = y
            else:
                acc[:, nn] += y
            return 0

        lax.fori_loop(0, 2 * C // TILE, tile, 0)

    def wait_pair(kind):
        for d in (0, 1):
            cnt = counts[(min(kind, 1), d)]
            for n in range(cnt):
                pairwise(1 - core, kind, d, n).wait_recv()

    wait_pair(0)
    matmul(0)
    matmul(1)
    for n in range(half):
        for d in (0, 1):
            if max(half - 2, 0) <= n < xcounts[d]:
                cross(2, d, n).wait_recv()
                go(pairwise(core, 2, d, n))
    wait_pair(1)
    matmul(2)
    matmul(3)
    wait_pair(2)
    matmul(4)
    matmul(5)

    for j in range(1, T):
        src = lax.rem(t - j + T, T)
        pltpu.make_async_remote_copy(
            src_ref=tg.at[src], dst_ref=tg.at[src], send_sem=ts.at[j], recv_sem=tr.at[j],
            device_id=(src, v), device_id_type=MESH).wait_recv()

    me = t * V + v
    base = me * C
    for q in range(T):
        rows = pl.ds(q * R, R)
        lp = acc[rows, pl.ds(0, C)]
        lr = acc[rows, pl.ds(C, C)]
        ids = lax.broadcasted_iota(jnp.int32, (R, C), 1) + base
        hit = ids == tg[q][:, 0:1]
        pp = jnp.max(lp, axis=1, keepdims=True)
        pr = jnp.max(lr, axis=1, keepdims=True)
        ep = jnp.exp(lp - pp)
        er_ = jnp.exp(lr - pr)
        parts = [
            pp, pr,
            jnp.sum(ep, axis=1, keepdims=True),
            jnp.sum(er_, axis=1, keepdims=True),
            jnp.sum(ep * (lp - lr), axis=1, keepdims=True),
            jnp.sum(jnp.where(hit, lp, 0.0), axis=1, keepdims=True),
            jnp.sum(jnp.where(hit, lr, 0.0), axis=1, keepdims=True),
        ]
        lane = lax.broadcasted_iota(jnp.int32, (R, 128), 1)
        s = jnp.zeros((R, 128), jnp.float32)
        for i, value in enumerate(parts):
            s = jnp.where(lane == i, value, s)
        s = jnp.concatenate([s, jnp.zeros((128 - R, 128), jnp.float32)], axis=0)
        st[q] = s.T[0:8, :]

    got[me] = st[t]

    def spread(j, _):
        q = lax.rem(me + j, T * V)
        qt, qv = q // V, lax.rem(q, V)
        pltpu.make_async_remote_copy(
            src_ref=st.at[qt], dst_ref=got.at[me], send_sem=es.at[j], recv_sem=er.at[j],
            device_id=(qt, qv), device_id_type=MESH).start()
        return 0

    lax.fori_loop(1, T * V, spread, 0)
    for cp in sends:
        cp.wait_send()

    def collect(j, _):
        q = lax.rem(me - j + T * V, T * V)
        cp = pltpu.make_async_remote_copy(
            src_ref=st.at[t], dst_ref=got.at[q], send_sem=es.at[j], recv_sem=er.at[j],
            device_id=(q // V, lax.rem(q, V)), device_id_type=MESH)
        cp.wait_recv()
        cp.wait_send()
        return 0

    lax.fori_loop(1, T * V, collect, 0)

    g = got[...]
    top = jnp.max(g, axis=0)
    scale = jnp.exp(g - top[None])
    pp, pr = top[0:1], top[1:2]
    sp, sr = scale[:, 0:1, :], scale[:, 1:2, :]
    tp = jnp.sum(g[:, 2:3, :] * sp, axis=0)
    tt = jnp.sum(g[:, 3:4, :] * sr, axis=0)
    wt = jnp.sum(g[:, 4:5, :] * sp, axis=0)
    hp = jnp.sum(g[:, 5:6, :], axis=0)
    hr = jnp.sum(g[:, 6:7, :], axis=0)
    np_ = pp + jnp.log(tp)
    nr = pr + jnp.log(tt)
    o0[...] = (hp - np_)[0, :R]
    o1[...] = (hr - nr)[0, :R]
    o2[...] = (wt / tp - np_ + nr)[0, :R]


def solution(mesh):
    T, V = mesh.shape["tok"], mesh.shape["vocab"]

    def body(hidden, policy_head, reference_head, targets):
        R, D = hidden.shape
        C = policy_head.shape[1]
        half = T // 2
        dma = pltpu.SemaphoreType.DMA
        anyspec = pl.BlockSpec(memory_space=pl.ANY)
        vm = pl.BlockSpec(memory_space=pltpu.VMEM)
        out = jax.ShapeDtypeStruct((R,), jnp.float32)
        return pl.pallas_call(
            functools.partial(kernel, T, V),
            out_shape=(out, out, out),
            in_specs=[anyspec, anyspec, anyspec, pl.BlockSpec(memory_space=pltpu.SMEM)],
            out_specs=(vm, vm, vm),
            scratch_shapes=[
                pltpu.VMEM((T, R, D), jnp.bfloat16),
                pltpu.VMEM((D, 2 * C), jnp.bfloat16),
                pltpu.VMEM((T * R, 2 * C), jnp.float32),
                pltpu.VMEM((T, R, 128), jnp.int32),
                pltpu.VMEM((T, 8, 128), jnp.float32),
                pltpu.VMEM((T * V, 8, 128), jnp.float32),
                dma((2, 6)),
                dma,
                dma((2, 2, half)),
                dma((2, 2, half)),
                dma((2, half)),
                dma((2, half)),
                dma((3, 2, half)),
                dma((3, 2, half)),
                dma((T,)),
                dma((T,)),
                dma((T * V,)),
                dma((T * V,)),
            ],
            compiler_params=pltpu.CompilerParams(
                collective_id=0, has_side_effects=True, vmem_limit_bytes=67043328),
        )(hidden, policy_head, reference_head, targets)

    in_specs = (P("tok", None), P(None, ("tok", "vocab")), P(None, ("tok", "vocab")), P("tok"))
    out_specs = (P("tok"), P("tok"), P("tok"))
    return jax.shard_map(body, mesh=mesh, in_specs=in_specs, out_specs=out_specs, check_vma=False)
```

time: 180 us -> 53.9 us (0.30)
  waiting for transfers between devices: 92.7 us -> 0 us
  Pallas kernels: 0 us -> 49.7 us
  starting transfers between devices: 23.1 us -> 0 us
  blocking collectives: 18.7 us -> 0 us
  matrix products: 15.6 us -> 0 us
  between operations: 15.5 us -> 0.64 us
  local copies, waits for them, and re-layouts: 12.7 us -> 3.42 us
    all_gather x1 -> x0, waiting for transfers between devices: 53.8 us -> none  [body(): piece = lax.all_gather(hidden, 'tok', axis=0, tiled=True)]
    pallas_call x0 -> x1, Pallas kernels: none -> 49.7 us  [body(): pl.pallas_call(functools.partial(kernel, T, V), out_shape=(out, out, out)...]
    all_to_all x7 -> x0, waiting for transfers between devices: 38.3 us -> none  [body(): lax.all_to_all(shaped, 'tok', split_axis=0, concat_axis=0, tiled=True)]
    all_to_all x7 -> x0, starting transfers between devices: 23 us -> none  [body(): lax.all_to_all(shaped, 'tok', split_axis=0, concat_axis=0, tiled=True)]
    unnamed x2 -> x0, blocking collectives: 18.7 us -> none
    dot_general x2 -> x0, matrix products: 15.6 us -> none  [the longest x1 9.63 us: body(): jnp.dot(piece, policy_head, preferred_element_type=jnp.float32)]
    all_to_all x7 -> x0, local copies, waits for them, and re-layouts: 4.75 us -> none  [body(): lax.all_to_all(shaped, 'tok', split_axis=0, concat_axis=0, tiled=True)]
    unnamed x22 -> x3, local copies, waits for them, and re-layouts: 7.34 us -> 3.42 us
  transfers between devices with their start and end apart: 8 -> 0, of which waited for: 8 -> 0; matrix products, arithmetic and copies ran while one was open for 2% -> 0% of each run, Pallas kernels for 0% -> 0%
where the time goes in v1:
time: 53.9 us; the launch traced here: 53.8 us
  Pallas kernels  49.7 us (92%)
  local copies, waits for them, and re-layouts  3.42 us (6%)
  between operations  0.64 us (1%)
    pallas_call x1, Pallas kernels, body(): pl.pallas_call(functools.partial(kernel, T, V), out_shape=(out, out, out)...  49.7 us
    unnamed x3, local copies, waits for them, and re-layouts  3.42 us

profile of v1, /device:TPU:0, one launch (start us, length us, event | category | flops | bytes accessed | tf_op | source)
XLA Modules:
  0.0 53.8 jit_solution(14022848084770178851)
XLA Ops:
  0.6 49.7 %shard_map.67 = (f32[24]{0:T(128)}, f32[24]{0:T(128)}, f32[24]{0:T(128)}) custom-call(bf16[24,9216]{1,0:T(8,128)(2,1)} %hid.1, bf16[9216,1024]{1,0:T(8,128)(2,1)} %wp.1, bf16[9216,1024]{1,0:T(8,128)(2,1)} %wr.1, s32[24]{0:T(128)} %tgt.1), custom_call_target="tpu_custom_call" | custom-call | tf_op jit(solution)/shard_map/pallas_call | solution.py:255
  50.3 1.1 %copy.10 = f32[24]{0:T(128)} copy(f32[24]{0:T(128)} %get-tuple-element.6) | data formatting | bytes 192
  51.4 1.1 %copy.11 = f32[24]{0:T(128)} copy(f32[24]{0:T(128)} %get-tuple-element.7) | data formatting | bytes 192
  52.6 1.2 %copy.12 = f32[24]{0:T(128)} copy(f32[24]{0:T(128)} %get-tuple-element.8) | data formatting | bytes 192

commit v2 on v1

--- a/solution.py
+++ b/solution.py
@@ -8,10 +8,10 @@
 from jax.sharding import PartitionSpec as P
 
 MESH = pl.DeviceIdType.MESH
-TILE = 256
-
-
-def kernel(T, V, hid, wp, wr, tgt, o0, o1, o2, h, w, acc, tg, st, got,
+TILE = 2048
+
+
+def kernel(T, V, hid, wp, wr, tgt, o, h, w, flat, acc, tg, st, got,
            wsem, osem, rs, rr, xs, xr, cs, cr, ts, tr, es, er):
     R = hid.shape[0]
     D = hid.shape[1]
@@ -38,7 +38,7 @@
             return 3 * c
         return 3 * c + 1 + (xb if kind == 1 else 1 - xb)
 
-    order = [(0, 0), (1, 0), (0, 1), (1, 1), (0, 2), (1, 2)]
+    order = [(core, 0), (core, 1), (1 - core, 0), (1 - core, 1), (core, 2), (1 - core, 2)]
 
     def cols(p):
         return pl.ds(pl.multiple_of(p * Kp, 128), Kp)
@@ -132,18 +132,21 @@
         k = cols(part(c, kind))
         for cp in wcopies[i]:
             cp.wait()
-        a = h[:, :, k].reshape(M, Kp)
+        for q in range(T):
+            flat[pl.ds(q * R, R), :] = h[q, :, k]
+
+        wide = min(TILE, 2 * C)
 
         def tile(j, _):
-            nn = pl.ds(pl.multiple_of(j * TILE, TILE), TILE)
-            y = jnp.dot(a, w[k, nn], preferred_element_type=jnp.float32)
+            nn = pl.ds(pl.multiple_of(j * wide, wide), wide)
+            y = jnp.dot(flat[...], w[k, nn], preferred_element_type=jnp.float32)
             if i == 0:
                 acc[:, nn] = y
             else:
                 acc[:, nn] += y
             return 0
 
-        lax.fori_loop(0, 2 * C // TILE, tile, 0)
+        lax.fori_loop(0, 2 * C // wide, tile, 0)
 
     def wait_pair(kind):
         for d in (0, 1):
@@ -151,19 +154,19 @@
             for n in range(cnt):
                 pairwise(1 - core, kind, d, n).wait_recv()
 
-    wait_pair(0)
     matmul(0)
-    matmul(1)
     for n in range(half):
         for d in (0, 1):
             if max(half - 2, 0) <= n < xcounts[d]:
                 cross(2, d, n).wait_recv()
                 go(pairwise(core, 2, d, n))
+    matmul(1)
+    wait_pair(0)
+    matmul(2)
     wait_pair(1)
-    matmul(2)
     matmul(3)
+    matmul(4)
     wait_pair(2)
-    matmul(4)
     matmul(5)
 
     for j in range(1, T):
@@ -236,9 +239,7 @@
     hr = jnp.sum(g[:, 6:7, :], axis=0)
     np_ = pp + jnp.log(tp)
     nr = pr + jnp.log(tt)
-    o0[...] = (hp - np_)[0, :R]
-    o1[...] = (hr - nr)[0, :R]
-    o2[...] = (wt / tp - np_ + nr)[0, :R]
+    o[...] = jnp.concatenate([hp - np_, hr - nr, wt / tp - np_ + nr], axis=0)
 
 
 def solution(mesh):
@@ -251,15 +252,16 @@
         dma = pltpu.SemaphoreType.DMA
         anyspec = pl.BlockSpec(memory_space=pl.ANY)
         vm = pl.BlockSpec(memory_space=pltpu.VMEM)
-        out = jax.ShapeDtypeStruct((R,), jnp.float32)
-        return pl.pallas_call(
+        out = jax.ShapeDtypeStruct((3, 128), jnp.float32)
+        o = pl.pallas_call(
             functools.partial(kernel, T, V),
-            out_shape=(out, out, out),
+            out_shape=out,
             in_specs=[anyspec, anyspec, anyspec, pl.BlockSpec(memory_space=pltpu.SMEM)],
-            out_specs=(vm, vm, vm),
+            out_specs=vm,
             scratch_shapes=[
                 pltpu.VMEM((T, R, D), jnp.bfloat16),
                 pltpu.VMEM((D, 2 * C), jnp.bfloat16),
+                pltpu.VMEM((T * R, D // 6), jnp.bfloat16),
                 pltpu.VMEM((T * R, 2 * C), jnp.float32),
                 pltpu.VMEM((T, R, 128), jnp.int32),
                 pltpu.VMEM((T, 8, 128), jnp.float32),
@@ -280,6 +282,7 @@
             compiler_params=pltpu.CompilerParams(
                 collective_id=0, has_side_effects=True, vmem_limit_bytes=67043328),
         )(hidden, policy_head, reference_head, targets)
+        return o[0, :R], o[1, :R], o[2, :R]
 
     in_specs = (P("tok", None), P(None, ("tok", "vocab")), P(None, ("tok", "vocab")), P("tok"))
     out_specs = (P("tok"), P("tok"), P("tok"))

time: 53.9 us -> 43.9 us (0.81)
  Pallas kernels: 49.7 us -> 41.8 us
  local copies, waits for them, and re-layouts: 3.42 us -> 1.3 us
    pallas_call x1, Pallas kernels: 49.7 us -> 41.8 us  [body(): pl.pallas_call(functools.partial(kernel, T, V), out_shape=out, in_specs=[...]
    unnamed x3 -> x0, local copies, waits for them, and re-layouts: 3.42 us -> none
    squeeze x0 -> x1, local copies, waits for them, and re-layouts: none -> 1.3 us  [body(): return (o[0, :R], o[1, :R], o[2, :R])]
where the time goes in v2:
time: 43.9 us; the launch traced here: 43.7 us
  Pallas kernels  41.8 us (95%)
  local copies, waits for them, and re-layouts  1.3 us (3%)
  between operations  0.64 us (1%)
    pallas_call x1, Pallas kernels, body(): pl.pallas_call(functools.partial(kernel, T, V), out_shape=out, in_specs=[...  41.8 us
    squeeze x1, local copies, waits for them, and re-layouts, body(): return (o[0, :R], o[1, :R], o[2, :R])  1.3 us

profile of v2, /device:TPU:0, one launch (start us, length us, event | category | flops | bytes accessed | tf_op | source)
XLA Modules:
  0.0 43.7 jit_solution(7909298316974598161)
XLA Ops:
  0.6 41.8 %shard_map.67 = f32[3,128]{1,0:T(4,128)} custom-call(bf16[24,9216]{1,0:T(8,128)(2,1)} %hid.1, bf16[9216,1024]{1,0:T(8,128)(2,1)} %wp.1, bf16[9216,1024]{1,0:T(8,128)(2,1)} %wr.1, s32[24]{0:T(128)} %tgt.1), custom_call_target="tpu_custom_call" | custom-call | tf_op jit(solution)/shard_map/pallas_call | solution.py:256
  42.4 1.3 %slice_bitcast_fusion = (f32[24]{0:T(128)}, f32[24]{0:T(128)}, f32[24]{0:T(128)}) fusion(f32[3,128]{1,0:T(4,128)} %shard_map.67), kind=kLoop, calls=%fused_computation | loop fusion | bytes 576 | tf_op jit(solution)/shard_map/squeeze | solution.py:285
